TPU v7x, 32 devices: a whole 2x2x4 slice. The times are simulated.
32 devices in a mesh: tm: 16 (over z, y, x), space: 2 (over core).
Axes of the slice: x: 2, y: 2, z: 4, core: 2. Of those that a mesh axis runs over, the one named last changes fastest.
Arguments:
- initial: float32 [16, 32, 64, 128], P('tm', 'space'), may hold values from -6 to 6
- source: float32 [16, 32, 64, 128], P('tm', 'space'), may hold values from -6 to 6
- diffusion: float32 [32, 64, 128], P('space'), may hold values from 0.1 to 1
- advection: float32 [3, 32, 64, 128], P(None, 'space'), may hold values from 0.05 to 0.5
Outputs:
- smoothed: float32 [16, 32, 64, 128], P('tm', 'space')
- residual: float32 [16, 32, 64, 128], P('tm', 'space')
All inputs are finite; a program needn't handle non-finite values.
Results may differ from a plain program's by a relative error of at most 0.00002.
Values sent between devices are 32-bit elements; how exact they have to be, the bound alone decides.
A program may use at most 64 MiB of HBM per device.

v0:
```python
import jax
import jax.numpy as jnp
from jax import lax
from jax.sharding import PartitionSpec as P

SWEEPS = 2
ITERS = 4


def from_behind(value, axis, steps):
    count = lax.axis_size(axis)
    pairs = [(source, (source + steps) % count) for source in range(count)]
    return lax.ppermute(value, axis, pairs)


def extended_2(value, sides, width):
    for axis, dim in sides:
        count, length = (lax.axis_size(axis), value.shape[dim])
        up = [(i, (i + 1) % count) for i in range(count - 1)]
        down = [(j, i) for i, j in up]
        last = lax.slice_in_dim(value, length - width, length, axis=dim)
        first = lax.slice_in_dim(value, 0, width, axis=dim)
        before = lax.ppermute(last, axis, up)
        after = lax.ppermute(first, axis, down)
        value = jnp.concatenate([before, value, after], axis=dim)
    return value


def off_terms(padded, spread, upwind):
    low_z = padded[..., :-2, 1:-1, 1:-1]
    high_z = padded[..., 2:, 1:-1, 1:-1]
    low_x = padded[..., 1:-1, :-2, 1:-1]
    high_x = padded[..., 1:-1, 2:, 1:-1]
    low_y = padded[..., 1:-1, 1:-1, :-2]
    high_y = padded[..., 1:-1, 1:-1, 2:]
    total = spread * (high_z + low_z + high_x + low_x + high_y + low_y)
    return total + upwind[0] * low_x + upwind[1] * low_y + upwind[2] * low_z


def main_diagonal(spread, upwind):
    return 1.0 + 6.0 * spread + (upwind[0] + upwind[1] + upwind[2])


def earlier_steps(field):
    arrived = from_behind(field, "tm", 1)
    return jnp.concatenate([arrived, field[:-1]], 0)


def body(initial, source, diffusion, advection):
    diagonal = main_diagonal(diffusion, advection)
    smoothed = initial
    coefs = jnp.concatenate([diffusion[None], advection], 0)
    wide_coefs = extended_2(coefs, (("space", 1),), ITERS)
    wide_spread = wide_coefs[0]
    wide_upwind = wide_coefs[1:]
    wide_diagonal = main_diagonal(wide_spread, wide_upwind)
    for sweep in range(SWEEPS):
        forcing = earlier_steps(smoothed) + source
        stacked = jnp.stack([smoothed, forcing], 0)
        widened = extended_2(stacked, (("space", 2),), ITERS)
        current = widened[0]
        wide_forcing = widened[1]
        for step in range(ITERS):
            padded = jnp.pad(current, ((0, 0), (1, 1), (1, 1), (1, 1)))
            current = (wide_forcing + off_terms(padded, wide_spread, wide_upwind)) / wide_diagonal
        smoothed = current[:, ITERS:-ITERS]
    prior = earlier_steps(smoothed)
    extended = extended_2(smoothed, (("space", 1),), 1)
    padded = jnp.pad(extended, ((0, 0), (0, 0), (1, 1), (1, 1)))
    applied = diagonal * smoothed - off_terms(padded, diffusion, advection)
    residual = source + prior - applied
    return (smoothed, residual)


def solution(mesh):
    in_specs = (
        P("tm", "space", None, None),
        P("tm", "space", None, None),
        P("space", None, None),
        P(None, "space", None, None),
    )
    out_specs = (P("tm", "space", None, None), P("tm", "space", None, None))
    return jax.shard_map(body, mesh=mesh, in_specs=in_specs, out_specs=out_specs, check_vma=False)
```

profile of v0, /device:TPU:0, one launch (start us, length us, event | category | flops | bytes accessed | tf_op | source)
XLA Modules:
  0.0 74.2 jit_solution(11025779953566761722)
XLA Ops:
  0.6 3.0 %collective-permute-start = (f32[1,16,64,128]{3,2,1,0:T(8,128)}, f32[1,16,64,128]{3,2,1,0:T(8,128)S(1)}, u32[]{:S(2)}, u32[]{:S(2)}) collective-permute-start(f32[1,16,64,128]{3,2,1,0:T(8,128)} %param.4), channel_id=1, source_target_pairs={{0,2},{2,4},{4,6},{6,8},{8,10},{10,12},{12,14},{14,16},{16,18},{18... | collective-permute-start | bytes 1572872 | tf_op jit(solution)/shard_map/ppermute | solution.py:13
  3.7 1.3 %pad_maximum_fusion.6 = (f32[4,4,64,128]{3,2,1,0:T(8,128)S(1)}, f32[4,4,64,128]{3,2,1,0:T(8,128)S(1)}) fusion(f32[3,16,64,128]{3,2,1,0:T(8,128)} %param.7, f32[1,16,64,128]{3,2,1,0:T(8,128)} %bitcast.38), kind=kLoop, calls=%fused_computation.170 | loop fusion | flops 262144 | bytes 3145728 | tf_op jit(solution)/shard_map/slice | solution.py:21
  5.0 1.6 %collective-permute-start.3 = (f32[4,4,64,128]{3,2,1,0:T(8,128)S(1)}, f32[4,4,64,128]{3,2,1,0:T(8,128)S(1)}, u32[]{:S(2)}, u32[]{:S(2)}) collective-permute-start(f32[4,4,64,128]{3,2,1,0:T(8,128)S(1)} %get-tuple-element.8), channel_id=1, source_target_pairs={{0,1},{2,3},{4,5},{6,7},{8,9},{10,11},{12,13},{14,15},{16,17},{18,... | collective-permute-start | bytes 1572872 | tf_op jit(solution)/shard_map/ppermute | solution.py:23
  6.6 1.4 %collective-permute-start.4 = (f32[4,4,64,128]{3,2,1,0:T(8,128)S(1)}, f32[4,4,64,128]{3,2,1,0:T(8,128)S(1)}, u32[]{:S(2)}, u32[]{:S(2)}) collective-permute-start(f32[4,4,64,128]{3,2,1,0:T(8,128)S(1)} %get-tuple-element.9), channel_id=1, source_target_pairs={{1,0},{3,2},{5,4},{7,6},{9,8},{11,10},{13,12},{15,14},{17,16},{19,... | collective-permute-start | bytes 1572872 | tf_op jit(solution)/shard_map/ppermute | solution.py:24
  8.1 11.7 %collective-permute-done = f32[1,16,64,128]{3,2,1,0:T(8,128)S(1)} collective-permute-done((f32[1,16,64,128]{3,2,1,0:T(8,128)}, f32[1,16,64,128]{3,2,1,0:T(8,128)S(1)}, u32[]{:S(2)}, u32[]{:S(2)}) %collective-permute-start) | collective-permute-done | bytes 524320 | tf_op jit(solution)/shard_map/ppermute | solution.py:13
  19.9 1.3 %collective-permute-start.1 = (f32[2,1,4,64,128]{4,3,2,1,0:T(8,128)S(1)}, f32[2,1,4,64,128]{4,3,2,1,0:T(8,128)S(1)}, u32[]{:S(2)}, u32[]{:S(2)}) collective-permute-start(f32[2,1,4,64,128]{4,3,2,1,0:T(8,128)S(1)} %get-tuple-element.14), channel_id=1, source_target_pairs={{0,1},{2,3},{4,5},{6,7},{8,9},{10,11},{12,13},{14,15},{16,17},{18,... | collective-permute-start | bytes 786440 | tf_op jit(solution)/shard_map/ppermute | solution.py:23
  21.2 1.3 %collective-permute-start.2 = (f32[2,1,4,64,128]{4,3,2,1,0:T(8,128)S(1)}, f32[2,1,4,64,128]{4,3,2,1,0:T(8,128)S(1)}, u32[]{:S(2)}, u32[]{:S(2)}) collective-permute-start(f32[2,1,4,64,128]{4,3,2,1,0:T(8,128)S(1)} %get-tuple-element.15), channel_id=1, source_target_pairs={{1,0},{3,2},{5,4},{7,6},{9,8},{11,10},{13,12},{15,14},{17,16},{19,... | collective-permute-start | bytes 786440 | tf_op jit(solution)/shard_map/ppermute | solution.py:24
  22.6 0.4 pad_maximum_fusion
  23.0 1.7 %collective-permute-done.2 = f32[2,1,4,64,128]{4,3,2,1,0:T(8,128)S(1)} collective-permute-done((f32[2,1,4,64,128]{4,3,2,1,0:T(8,128)S(1)}, f32[2,1,4,64,128]{4,3,2,1,0:T(8,128)S(1)}, u32[]{:S(2)}, u32[]{:S(2)}) %collective-permute-start.2) | collective-permute-done | bytes 262176 | tf_op jit(solution)/shard_map/ppermute | solution.py:24
  24.6 0.1 pad_maximum_fusion.1
  24.7 0.2 slice_bitcast_fusion.2
  24.9 1.2 %fusion.97 = (f32[1,24,64,128]{3,2,1,0:T(8,128)S(1)}, f32[1,24,64,128]{3,2,1,0:T(8,128)S(1)}, f32[1,24,64,128]{3,2,1,0:T(8,128)S(1)}, f32[1,24,64,128]{3,2,1,0:T...) fusion(f32[4,24,64,128]{3,2,1,0:T(8,128)S(1)} %pad_maximum_fusion, ...), kind=kLoop, calls=%fused_computation.179 | loop fusion | flops 3735552 | bytes 9437184 | tf_op jit(solution)/shard_map/slice | solution.py:54
  26.1 0.8 %fusion.24 = f32[1,24,64,128]{3,2,1,0:T(8,128)S(1)} fusion(f32[1,24,64,128]{3,2,1,0:T(8,128)S(1)} %get-tuple-element.3, f32[2,1,24,64,128]{4,3,2,1,0:T(8,128)S(1)} %pad_maximum_fusion.1, f32[4,24,64,128]{3,2,1,0:T(8,128)S(1)} %pad_maximum_fusion), kind=kLoop, calls=%fused_computation.81 | loop fusion | flops 3735552 | bytes 5505024 | tf_op jit(solution)/shard_map/div | solution.py:65
  26.9 0.8 %fusion.35 = f32[1,24,64,128]{3,2,1,0:T(8,128)S(1)} fusion(f32[1,24,64,128]{3,2,1,0:T(8,128)S(1)} %fusion.24, f32[2,1,24,64,128]{4,3,2,1,0:T(8,128)S(1)} %pad_maximum_fusion.1, f32[4,24,64,128]{3,2,1,0:T(8,128)S(1)} %pad_maximum_fusion), kind=kLoop, calls=%fused_computation.92 | loop fusion | flops 3735552 | bytes 5505024 | tf_op jit(solution)/shard_map/div | solution.py:65
  27.7 0.8 %fusion.40 = (f32[1,24,64,128]{3,2,1,0:T(8,128)S(1)}, f32[1,24,64,128]{3,2,1,0:T(8,128)S(1)}, f32[1,24,64,128]{3,2,1,0:T(8,128)S(1)}, f32[1,24,64,128]{3,2,1,0:T(8,128)S(1)}) fusion(f32[1,24,64,128]{3,2,1,0:T(8,128)S(1)} %fusion.35), kind=kLoop, calls=%fused_computation.97 | loop fusion | flops 983040 | bytes 3932160 | tf_op jit(solution)/shard_map/add | solution.py:36
  28.5 0.5 slice_divide_fusion
  29.2 17.5 %collective-permute-done.5 = f32[1,16,64,128]{3,2,1,0:T(8,128)S(1)} collective-permute-done((f32[1,16,64,128]{3,2,1,0:T(8,128)S(1)}, f32[1,16,64,128]{3,2,1,0:T(8,128)S(1)}, u32[]{:S(2)}, u32[]{:S(2)}) %collective-permute-start.5) | collective-permute-done | bytes 524320 | tf_op jit(solution)/shard_map/ppermute | solution.py:13
  46.8 1.3 %collective-permute-start.6 = (f32[2,1,4,64,128]{4,3,2,1,0:T(8,128)S(1)}, f32[2,1,4,64,128]{4,3,2,1,0:T(8,128)S(1)}, u32[]{:S(2)}, u32[]{:S(2)}) collective-permute-start(f32[2,1,4,64,128]{4,3,2,1,0:T(8,128)S(1)} %get-tuple-element.12), channel_id=1, source_target_pairs={{0,1},{2,3},{4,5},{6,7},{8,9},{10,11},{12,13},{14,15},{16,17},{18,... | collective-permute-start | bytes 786440 | tf_op jit(solution)/shard_map/ppermute | solution.py:23
  48.1 1.3 %collective-permute-start.7 = (f32[2,1,4,64,128]{4,3,2,1,0:T(8,128)S(1)}, f32[2,1,4,64,128]{4,3,2,1,0:T(8,128)S(1)}, u32[]{:S(2)}, u32[]{:S(2)}) collective-permute-start(f32[2,1,4,64,128]{4,3,2,1,0:T(8,128)S(1)} %get-tuple-element.13), channel_id=1, source_target_pairs={{1,0},{3,2},{5,4},{7,6},{9,8},{11,10},{13,12},{15,14},{17,16},{19,... | collective-permute-start | bytes 786440 | tf_op jit(solution)/shard_map/ppermute | solution.py:24
  49.5 2.1 %collective-permute-done.7 = f32[2,1,4,64,128]{4,3,2,1,0:T(8,128)S(1)} collective-permute-done((f32[2,1,4,64,128]{4,3,2,1,0:T(8,128)S(1)}, f32[2,1,4,64,128]{4,3,2,1,0:T(8,128)S(1)}, u32[]{:S(2)}, u32[]{:S(2)}) %collective-permute-start.7) | collective-permute-done | bytes 262176 | tf_op jit(solution)/shard_map/ppermute | solution.py:24
  51.6 0.1 pad_maximum_fusion.2
  51.7 0.8 %fusion.51 = f32[1,24,64,128]{3,2,1,0:T(8,128)S(1)} fusion(f32[1,24,64,128]{3,2,1,0:T(8,128)S(1)} %slice_bitcast_fusion, f32[2,1,24,64,128]{4,3,2,1,0:T(8,128)S(1)} %pad_maximum_fusion.2, f32[4,24,64,128]{3,2,1,0:T(8,128)S(1)} %pad_maximum_fusion), kind=kLoop, calls=%fused_computation.108 | loop fusion | flops 3735552 | bytes 5505024 | tf_op jit(solution)/shard_map/div | solution.py:65
  52.5 0.8 %fusion.62 = f32[1,24,64,128]{3,2,1,0:T(8,128)S(1)} fusion(f32[1,24,64,128]{3,2,1,0:T(8,128)S(1)} %fusion.51, f32[2,1,24,64,128]{4,3,2,1,0:T(8,128)S(1)} %pad_maximum_fusion.2, f32[4,24,64,128]{3,2,1,0:T(8,128)S(1)} %pad_maximum_fusion), kind=kLoop, calls=%fused_computation.119 | loop fusion | flops 3735552 | bytes 5505024 | tf_op jit(solution)/shard_map/div | solution.py:65
  53.4 0.8 %fusion.73 = f32[1,24,64,128]{3,2,1,0:T(8,128)S(1)} fusion(f32[1,24,64,128]{3,2,1,0:T(8,128)S(1)} %fusion.62, f32[2,1,24,64,128]{4,3,2,1,0:T(8,128)S(1)} %pad_maximum_fusion.2, f32[4,24,64,128]{3,2,1,0:T(8,128)S(1)} %pad_maximum_fusion), kind=kLoop, calls=%fused_computation.130 | loop fusion | flops 3735552 | bytes 5505024 | tf_op jit(solution)/shard_map/div | solution.py:65
  54.2 0.8 %fusion.84 = f32[1,24,64,128]{3,2,1,0:T(8,128)S(1)} fusion(f32[1,24,64,128]{3,2,1,0:T(8,128)S(1)} %fusion.73, f32[2,1,24,64,128]{4,3,2,1,0:T(8,128)S(1)} %pad_maximum_fusion.2, f32[4,24,64,128]{3,2,1,0:T(8,128)S(1)} %pad_maximum_fusion), kind=kLoop, calls=%fused_computation.141 | loop fusion | flops 3735552 | bytes 5505024 | tf_op jit(solution)/shard_map/div | solution.py:65
  55.0 0.1 collective-permute-start.8
  55.1 2.0 %collective-permute-start.10 = (f32[1,1,64,128]{3,2,1,0:T(8,128)S(1)}, f32[1,1,64,128]{3,2,1,0:T(8,128)S(1)}, u32[]{:S(2)}, u32[]{:S(2)}) collective-permute-start(f32[1,1,64,128]{3,2,1,0:T(8,128)S(1)} %get-tuple-element.16), channel_id=1, source_target_pairs={{0,1},{2,3},{4,5},{6,7},{8,9},{10,11},{12,13},{14,15},{16,17},{18,... | collective-permute-start | bytes 98312 | tf_op jit(solution)/shard_map/ppermute | solution.py:23
  57.2 1.3 %collective-permute-start.9 = (f32[1,1,64,128]{3,2,1,0:T(8,128)S(1)}, f32[1,1,64,128]{3,2,1,0:T(8,128)S(1)}, u32[]{:S(2)}, u32[]{:S(2)}) collective-permute-start(f32[1,1,64,128]{3,2,1,0:T(8,128)S(1)} %get-tuple-element.17), channel_id=1, source_target_pairs={{1,0},{3,2},{5,4},{7,6},{9,8},{11,10},{13,12},{15,14},{17,16},{19,... | collective-permute-start | bytes 98312 | tf_op jit(solution)/shard_map/ppermute | solution.py:24
  58.5 1.8 %collective-permute-done.9 = f32[1,1,64,128]{3,2,1,0:T(8,128)S(1)} collective-permute-done((f32[1,1,64,128]{3,2,1,0:T(8,128)S(1)}, f32[1,1,64,128]{3,2,1,0:T(8,128)S(1)}, u32[]{:S(2)}, u32[]{:S(2)}) %collective-permute-start.9) | collective-permute-done | bytes 32800 | tf_op jit(solution)/shard_map/ppermute | solution.py:24
  60.3 0.4 select_maximum_fusion
  60.7 12.0 %collective-permute-done.8 = f32[1,16,64,128]{3,2,1,0:T(8,128)S(1)} collective-permute-done((f32[1,16,64,128]{3,2,1,0:T(8,128)S(1)}, f32[1,16,64,128]{3,2,1,0:T(8,128)S(1)}, u32[]{:S(2)}, u32[]{:S(2)}) %collective-permute-start.8) | collective-permute-done | bytes 524320 | tf_op jit(solution)/shard_map/ppermute | solution.py:13
  72.7 1.5 %fusion.91 = f32[1,16,64,128]{3,2,1,0:T(8,128)} fusion(f32[1,18,66,130]{3,2,1,0:T(8,128)S(1)} %select_maximum_fusion, f32[1,1,64,128]{3,2,1,0:T(8,128)S(1)} %collective-permute-done.9, f32[1,16,64,128]{3,2,1,0:T(8,128)S(1)} %slice.355, f32[1,1,64,128]{3,2,1,0:T(8,128)S(1)} %collective-permute-done.10, f32[3,16,64,128]{3,2,1,0:T(8,128)S(1)} %copy-done, ...), kind=kLoop, calls=%fused_computation.154 | loop fusion | flops 3014656 | bytes 6356992 | tf_op jit(solution)/shard_map/sub | solution.py:71
  (23 shorter events, 0.4 us)
Async XLA Ops:
  0.6 19.1 %collective-permute-start = (f32[1,16,64,128]{3,2,1,0:T(8,128)}, f32[1,16,64,128]{3,2,1,0:T(8,128)S(1)}, u32[]{:S(2)}, u32[]{:S(2)}) collective-permute-start(f32[1,16,64,128]{3,2,1,0:T(8,128)} %param.4), channel_id=1, source_target_pairs={{0,2},{2,4},{4,6},{6,8},{8,10},{10,12},{12,14},{14,16},{16,18},{18... | collective-permute-start | bytes 1572872 | tf_op jit(solution)/shard_map/ppermute | solution.py:13
  3.6 16.1 %copy-start.1 = (f32[1,16,64,128]{3,2,1,0:T(8,128)S(1)}, f32[1,16,64,128]{3,2,1,0:T(8,128)}, u32[]{:S(2)}) copy-start(f32[1,16,64,128]{3,2,1,0:T(8,128)} %param.5) | copy-start | bytes 1572868
  5.0 14.9 %copy-start.4 = (f32[1,16,64,128]{3,2,1,0:T(8,128)S(1)}, f32[1,16,64,128]{3,2,1,0:T(8,128)}, u32[]{:S(2)}) copy-start(f32[1,16,64,128]{3,2,1,0:T(8,128)} %param.4) | copy-start | bytes 1572868
  5.0 17.5 %collective-permute-start.3 = (f32[4,4,64,128]{3,2,1,0:T(8,128)S(1)}, f32[4,4,64,128]{3,2,1,0:T(8,128)S(1)}, u32[]{:S(2)}, u32[]{:S(2)}) collective-permute-start(f32[4,4,64,128]{3,2,1,0:T(8,128)S(1)} %get-tuple-element.8), channel_id=1, source_target_pairs={{0,1},{2,3},{4,5},{6,7},{8,9},{10,11},{12,13},{14,15},{16,17},{18,... | collective-permute-start | bytes 1572872 | tf_op jit(solution)/shard_map/ppermute | solution.py:23
  6.6 15.9 %copy-start = (f32[3,16,64,128]{3,2,1,0:T(8,128)S(1)}, f32[3,16,64,128]{3,2,1,0:T(8,128)}, u32[]{:S(2)}) copy-start(f32[3,16,64,128]{3,2,1,0:T(8,128)} %param.7) | copy-start | bytes 4718596
  6.6 15.9 %copy-start.2 = (f32[16,64,128]{2,1,0:T(8,128)S(1)}, f32[16,64,128]{2,1,0:T(8,128)}, u32[]{:S(2)}) copy-start(f32[16,64,128]{2,1,0:T(8,128)} %param.6) | copy-start | bytes 1572868
  6.6 15.9 %collective-permute-start.4 = (f32[4,4,64,128]{3,2,1,0:T(8,128)S(1)}, f32[4,4,64,128]{3,2,1,0:T(8,128)S(1)}, u32[]{:S(2)}, u32[]{:S(2)}) collective-permute-start(f32[4,4,64,128]{3,2,1,0:T(8,128)S(1)} %get-tuple-element.9), channel_id=1, source_target_pairs={{1,0},{3,2},{5,4},{7,6},{9,8},{11,10},{13,12},{15,14},{17,16},{19,... | collective-permute-start | bytes 1572872 | tf_op jit(solution)/shard_map/ppermute | solution.py:24
  19.9 3.1 %collective-permute-start.1 = (f32[2,1,4,64,128]{4,3,2,1,0:T(8,128)S(1)}, f32[2,1,4,64,128]{4,3,2,1,0:T(8,128)S(1)}, u32[]{:S(2)}, u32[]{:S(2)}) collective-permute-start(f32[2,1,4,64,128]{4,3,2,1,0:T(8,128)S(1)} %get-tuple-element.14), channel_id=1, source_target_pairs={{0,1},{2,3},{4,5},{6,7},{8,9},{10,11},{12,13},{14,15},{16,17},{18,... | collective-permute-start | bytes 786440 | tf_op jit(solution)/shard_map/ppermute | solution.py:23
  21.2 3.4 %collective-permute-start.2 = (f32[2,1,4,64,128]{4,3,2,1,0:T(8,128)S(1)}, f32[2,1,4,64,128]{4,3,2,1,0:T(8,128)S(1)}, u32[]{:S(2)}, u32[]{:S(2)}) collective-permute-start(f32[2,1,4,64,128]{4,3,2,1,0:T(8,128)S(1)} %get-tuple-element.15), channel_id=1, source_target_pairs={{1,0},{3,2},{5,4},{7,6},{9,8},{11,10},{13,12},{15,14},{17,16},{19,... | collective-permute-start | bytes 786440 | tf_op jit(solution)/shard_map/ppermute | solution.py:24
  29.1 17.6 %collective-permute-start.5 = (f32[1,16,64,128]{3,2,1,0:T(8,128)S(1)}, f32[1,16,64,128]{3,2,1,0:T(8,128)S(1)}, u32[]{:S(2)}, u32[]{:S(2)}) collective-permute-start(f32[1,16,64,128]{3,2,1,0:T(8,128)S(1)} %slice_divide_fusion), channel_id=1, source_target_pairs={{0,2},{2,4},{4,6},{6,8},{8,10},{10,12},{12,14},{14,16},{16,18},{18... | collective-permute-start | bytes 1572872 | tf_op jit(solution)/shard_map/ppermute | solution.py:13
  46.8 2.6 %collective-permute-start.6 = (f32[2,1,4,64,128]{4,3,2,1,0:T(8,128)S(1)}, f32[2,1,4,64,128]{4,3,2,1,0:T(8,128)S(1)}, u32[]{:S(2)}, u32[]{:S(2)}) collective-permute-start(f32[2,1,4,64,128]{4,3,2,1,0:T(8,128)S(1)} %get-tuple-element.12), channel_id=1, source_target_pairs={{0,1},{2,3},{4,5},{6,7},{8,9},{10,11},{12,13},{14,15},{16,17},{18,... | collective-permute-start | bytes 786440 | tf_op jit(solution)/shard_map/ppermute | solution.py:23
  48.1 3.4 %collective-permute-start.7 = (f32[2,1,4,64,128]{4,3,2,1,0:T(8,128)S(1)}, f32[2,1,4,64,128]{4,3,2,1,0:T(8,128)S(1)}, u32[]{:S(2)}, u32[]{:S(2)}) collective-permute-start(f32[2,1,4,64,128]{4,3,2,1,0:T(8,128)S(1)} %get-tuple-element.13), channel_id=1, source_target_pairs={{1,0},{3,2},{5,4},{7,6},{9,8},{11,10},{13,12},{15,14},{17,16},{19,... | collective-permute-start | bytes 786440 | tf_op jit(solution)/shard_map/ppermute | solution.py:24
  55.0 19.2 %copy-start.3 = (f32[1,16,64,128]{3,2,1,0:T(8,128)}, f32[1,16,64,128]{3,2,1,0:T(8,128)S(1)}, u32[]{:S(2)}) copy-start(f32[1,16,64,128]{3,2,1,0:T(8,128)S(1)} %slice.355) | copy-start | bytes 1572868
  55.0 17.6 %collective-permute-start.8 = (f32[1,16,64,128]{3,2,1,0:T(8,128)S(1)}, f32[1,16,64,128]{3,2,1,0:T(8,128)S(1)}, u32[]{:S(2)}, u32[]{:S(2)}) collective-permute-start(f32[1,16,64,128]{3,2,1,0:T(8,128)S(1)} %slice.355), channel_id=1, source_target_pairs={{0,2},{2,4},{4,6},{6,8},{8,10},{10,12},{12,14},{14,16},{16,18},{18... | collective-permute-start | bytes 1572872 | tf_op jit(solution)/shard_map/ppermute | solution.py:13
  55.1 3.4 %collective-permute-start.10 = (f32[1,1,64,128]{3,2,1,0:T(8,128)S(1)}, f32[1,1,64,128]{3,2,1,0:T(8,128)S(1)}, u32[]{:S(2)}, u32[]{:S(2)}) collective-permute-start(f32[1,1,64,128]{3,2,1,0:T(8,128)S(1)} %get-tuple-element.16), channel_id=1, source_target_pairs={{0,1},{2,3},{4,5},{6,7},{8,9},{10,11},{12,13},{14,15},{16,17},{18,... | collective-permute-start | bytes 98312 | tf_op jit(solution)/shard_map/ppermute | solution.py:23
  57.2 3.1 %collective-permute-start.9 = (f32[1,1,64,128]{3,2,1,0:T(8,128)S(1)}, f32[1,1,64,128]{3,2,1,0:T(8,128)S(1)}, u32[]{:S(2)}, u32[]{:S(2)}) collective-permute-start(f32[1,1,64,128]{3,2,1,0:T(8,128)S(1)} %get-tuple-element.17), channel_id=1, source_target_pairs={{1,0},{3,2},{5,4},{7,6},{9,8},{11,10},{13,12},{15,14},{17,16},{19,... | collective-permute-start | bytes 98312 | tf_op jit(solution)/shard_map/ppermute | solution.py:24
where the time goes:
time: 74.5 us; the launch traced here: 74.2 us
  waiting for transfers between devices  46.8 us (63%)
  starting transfers between devices  14.7 us (20%)
  other arithmetic  11.4 us (15%)
  between operations  0.94 us (1%)
    ppermute x3, waiting for transfers between devices, from_behind(): return lax.ppermute(value, axis, pairs)  41.2 us
    ppermute x4, starting transfers between devices, extended_2(): before = lax.ppermute(last, axis, up)  6.28 us
    ppermute x4, waiting for transfers between devices, extended_2(): after = lax.ppermute(first, axis, down)  5.58 us
    div x7, other arithmetic, body(): (wide_forcing + off_terms(padded, wide_spread, wide_upwind)) / wide_diagonal  5.41 us
    ppermute x4, starting transfers between devices, extended_2(): after = lax.ppermute(first, axis, down)  5.3 us
    ppermute x3, starting transfers between devices, from_behind(): return lax.ppermute(value, axis, pairs)  3.14 us
    sub x1, other arithmetic, body(): residual = source + prior - applied  1.53 us
  transfers between devices with their start and end apart: 11, of which 6 were waited for; matrix products, arithmetic and copies ran while one was open for 3% of the time, Pallas kernels for 0%

commit v1 on v0

v1 whole, which is shorter than its diff:
```python
import functools

import jax
import jax.numpy as jnp
from jax import lax
from jax.experimental import pallas as pl
from jax.experimental.pallas import tpu as pltpu
from jax.sharding import PartitionSpec as P

SWEEPS = 2
ITERS = 4
HALO = ITERS
MESH = pl.DeviceIdType.MESH


def cuts(edges):
    return list(zip(edges[:-1], edges[1:]))


def plan(planes, step):
    arrive = list(range(0, planes, step)) + [planes]
    ready = lambda edges: [e if e == planes else max(e - (ITERS - 1), 0) for e in edges]
    split = lambda edges, most: sorted({c for a, b in cuts(edges) for c in list(range(a, b, most)) + [b]})
    first = cuts(arrive)
    second = cuts(split(sorted(set(ready(arrive))), step))
    edges = [0] + [b for _, b in second]
    third = cuts(split(sorted(set(ready(edges))), 2))
    return first, second, third


def kernel(planes, steps, sends, initial, source, diffusion, advection, smoothed, residual,
           v0, v1, v2, v3, s1, s2, src, p1, p2, p3, spread, upwind,
           low_z, high_z, low_x, high_x, low_y, high_y, inverse, diagonal, forced, left,
           load_sem, out_sem, send1, recv1, send2, recv2, send3, recv3, hsend, hrecv):
    first, second, third = sends
    time, side = lax.axis_index("tm"), lax.axis_index("space")
    after, before = lax.rem(time + 1, steps), lax.rem(time + steps - 1, steps)
    other = 1 - side
    rows, lanes = v0.shape[1], v0.shape[2]

    def begin(lo, hi, who=side):
        return who * (HALO + lo) + (1 - who) * (HALO + planes - hi)

    def span(lo, hi, who=side):
        return pl.ds(begin(lo, hi, who), hi - lo)

    def grid_span(lo, hi):
        return pl.ds(begin(lo, hi) - HALO, hi - lo)

    barrier = pltpu.get_barrier_semaphore()
    for peer in ((after, side), (before, side), (time, other)):
        pl.semaphore_signal(barrier, inc=1, device_id=peer, device_id_type=MESH)

    inner = pl.ds(HALO, planes)
    loads = [
        pltpu.make_async_copy(diffusion, spread.at[inner], load_sem.at[0]),
        pltpu.make_async_copy(advection, upwind.at[:, inner], load_sem.at[1]),
        pltpu.make_async_copy(source.at[0], src.at[inner], load_sem.at[2]),
        pltpu.make_async_copy(initial.at[0], v0.at[inner], load_sem.at[3]),
    ]
    for load in loads:
        load.start()

    edge = begin(planes, planes + 1)
    for field in (v0, v1, v2, v3, s1, s2):
        field[edge] = jnp.zeros((rows, lanes), jnp.float32)

    def forward(source_ref, target_ref, send, recv):
        return pltpu.make_async_remote_copy(
            src_ref=source_ref, dst_ref=target_ref, send_sem=send, recv_sem=recv,
            device_id=(after, side), device_id_type=MESH)

    def across(source_ref, target_ref, n):
        return pltpu.make_async_remote_copy(
            src_ref=source_ref, dst_ref=target_ref, send_sem=hsend.at[n], recv_sem=hrecv.at[n],
            device_id=(time, other), device_id_type=MESH)

    def rim(field, width, n):
        return across(field.at[span(0, width)], field.at[span(-width, 0, other)], n)

    near = HALO - 1
    sent1 = [
        forward(initial.at[0, grid_span(lo, hi)], p1.at[span(lo, hi)], send1.at[k], recv1.at[k])
        for k, (lo, hi) in enumerate(first)
    ]
    sent2 = [
        forward(s1.at[span(lo, hi)], p2.at[span(lo, hi)], send2.at[k], recv2.at[k])
        for k, (lo, hi) in enumerate(second)
    ]
    sent3 = [
        forward(s2.at[span(lo, hi)], p3.at[span(lo, hi)], send3.at[k], recv3.at[k])
        for k, (lo, hi) in enumerate(third)
    ]
    rims = [
        across(diffusion.at[grid_span(0, near)], spread.at[span(-near, 0, other)], 0),
        across(advection.at[:, grid_span(0, near)], upwind.at[:, span(-near, 0, other)], 1),
        across(source.at[0, grid_span(0, near)], src.at[span(-near, 0, other)], 2),
        across(initial.at[0, grid_span(0, HALO)], v0.at[span(-HALO, 0, other)], 3),
    ]
    rim_p1, rim_s1, rim_p2, rim_s2 = rim(p1, near, 4), rim(s1, HALO, 5), rim(p2, near, 6), rim(s2, 1, 7)

    pl.semaphore_wait(barrier, 3)
    sent1[0].start()
    for copy in rims:
        copy.start()
    for copy in sent1[1:]:
        copy.start()

    def each(lo, hi, body):
        if hi > lo:
            start = begin(lo, hi)

            def one(k, carry):
                body(start + k)
                return carry

            lax.fori_loop(0, hi - lo, one, 0)

    def coefficients(i):
        d = spread[i]
        ax, ay, az = upwind[0, i], upwind[1, i], upwind[2, i]
        main = 1.0 + 6.0 * d + (ax + ay + az)
        inv = 1.0 / main
        row = lax.broadcasted_iota(jnp.int32, (rows, lanes), 0)
        lane = lax.broadcasted_iota(jnp.int32, (rows, lanes), 1)
        even = d * inv
        high_z[i] = even
        low_z[i] = (d + az) * inv
        high_x[i] = jnp.where(row == rows - 1, 0.0, even)
        low_x[i] = jnp.where(row == 0, 0.0, (d + ax) * inv)
        high_y[i] = jnp.where(lane == lanes - 1, 0.0, even)
        low_y[i] = jnp.where(lane == 0, 0.0, (d + ay) * inv)
        inverse[i] = inv
        diagonal[i] = main

    def neighbours(v, i):
        here = v[i]
        total = low_z[i] * v[i - 1] + high_z[i] * v[i + 1]
        total += low_x[i] * pltpu.roll(here, 1, 0) + high_x[i] * pltpu.roll(here, rows - 1, 0)
        return total + (low_y[i] * pltpu.roll(here, 1, 1) + high_y[i] * pltpu.roll(here, lanes - 1, 1))

    def sweep(start, target, prior, arrivals, ranges, rim_prior, on_ready):
        levels = [start, v1, v2, v3, target]
        reached = [-near] + [-(ITERS - n) for n in range(1, ITERS + 1)]
        rimmed = False
        for k, (lo, hi) in enumerate(ranges):
            arrivals[k].wait_recv()
            if hi < near:
                continue
            if not rimmed:
                rim_prior.start()
                rim_prior.wait_recv()
                rimmed = True
            goal = hi

            def force(i):
                forced[i] = (prior[i] + src[i]) * inverse[i]

            each(reached[0], goal, force)
            reached[0] = goal
            for n in range(1, ITERS + 1):
                goal = hi if hi == planes else hi - (n - 1)

                def iterate(i, n=n):
                    levels[n][i] = forced[i] + neighbours(levels[n - 1], i)

                each(reached[n], goal, iterate)
                reached[n] = max(reached[n], goal)
            on_ready(reached[ITERS])

    for n in (0, 1):
        loads[n].wait()
        rims[n].wait_recv()
    each(-near, planes, coefficients)
    for n in (2, 3):
        loads[n].wait()
        rims[n].wait_recv()

    issued = {"s1": 0, "s2": 0, "rim": set()}

    def issue(name, copies, ranges, ready, extra=None):
        while issued[name] < len(ranges) and ranges[issued[name]][1] <= ready:
            copies[issued[name]].start()
            if extra is not None:
                extra[issued[name]].start()
            issued[name] += 1

    def first_ready(ready):
        if ready >= HALO and "s1" not in issued["rim"]:
            issued["rim"].add("s1")
            rim_s1.start()
        issue("s1", sent2, second, ready)

    outs = [
        pltpu.make_async_copy(s2.at[span(lo, hi)], smoothed.at[0, grid_span(lo, hi)], out_sem.at[0, k])
        for k, (lo, hi) in enumerate(third)
    ]

    def second_ready(ready):
        if ready >= 1 and "s2" not in issued["rim"]:
            issued["rim"].add("s2")
            rim_s2.start()
        issue("s2", sent3, third, ready, outs)

    sweep(v0, s1, p1, sent1, first, rim_p1, first_ready)
    rim_s1.wait_recv()
    sweep(s1, s2, p2, sent2, second, rim_p2, second_ready)
    rim_s2.wait_recv()

    def partial(i):
        left[i] = src[i] - diagonal[i] * (s2[i] - neighbours(s2, i))

    each(0, planes, partial)

    ends = [
        pltpu.make_async_copy(left.at[span(lo, hi)], residual.at[0, grid_span(lo, hi)], out_sem.at[1, k])
        for k, (lo, hi) in enumerate(third)
    ]
    for k, (lo, hi) in enumerate(third):
        sent3[k].wait_recv()

        def finish(i):
            left[i] = left[i] + p3[i]

        each(lo, hi, finish)
        ends[k].start()

    for copy in rims + [rim_p1, rim_s1, rim_p2, rim_s2] + sent1 + sent2 + sent3:
        copy.wait_send()
    for copy in outs + ends:
        copy.wait()


def body(steps, sides, initial, source, diffusion, advection):
    assert sides == 2
    _, planes, rows, lanes = initial.shape
    sends = plan(planes, 4)
    most = max(len(s) for s in sends)
    wide = pltpu.VMEM((planes + 2 * HALO, rows, lanes), jnp.float32)
    triple = pltpu.VMEM((3, planes + 2 * HALO, rows, lanes), jnp.float32)
    dma = pltpu.SemaphoreType.DMA
    pairs = [dma((len(s),)) for s in sends for _ in range(2)]
    result = jax.ShapeDtypeStruct(initial.shape, jnp.float32)
    return pl.pallas_call(
        functools.partial(kernel, planes, steps, sends),
        out_shape=(result, result),
        in_specs=[pl.BlockSpec(memory_space=pl.ANY)] * 4,
        out_specs=(pl.BlockSpec(memory_space=pl.ANY),) * 2,
        scratch_shapes=[wide] * 11 + [triple] + [wide] * 10
        + [dma((4,)), dma((2, most))] + pairs + [dma((8,)), dma((8,))],
        compiler_params=pltpu.CompilerParams(collective_id=0, has_side_effects=True),
        name="smooth",
    )(initial, source, diffusion, advection)


def solution(mesh):
    in_specs = (
        P("tm", "space", None, None),
        P("tm", "space", None, None),
        P("space", None, None),
        P(None, "space", None, None),
    )
    out_specs = (P("tm", "space", None, None), P("tm", "space", None, None))
    run = functools.partial(body, mesh.shape["tm"], mesh.shape["space"])
    return jax.shard_map(run, mesh=mesh, in_specs=in_specs, out_specs=out_specs, check_vma=False)
```

time: 74.5 us -> 48.2 us (0.65)
  waiting for transfers between devices: 46.8 us -> 0 us
  Pallas kernels: 0 us -> 43.5 us
  starting transfers between devices: 14.7 us -> 0 us
  other arithmetic: 11.4 us -> 0 us
  local copies, waits for them, and re-layouts: 0.29 us -> 3.77 us
    ppermute x11 -> x0, waiting for transfers between devices: 46.8 us -> none  [the longest x3 41.2 us: from_behind(): return lax.ppermute(value, axis, pairs)]
    pallas_call x0 -> x1, Pallas kernels: none -> 43.5 us  [body(): pl.pallas_call(functools.partial(kernel, planes, steps, sends), out_shape...]
    ppermute x11 -> x0, starting transfers between devices: 14.7 us -> none  [the longest x4 6.28 us: extended_2(): before = lax.ppermute(last, axis, up)]
    div x7 -> x0, other arithmetic: 5.41 us -> none  [body(): (wide_forcing + off_terms(padded, wide_spread, wide_upwind)) / wide_diagonal]
    unnamed x10 -> x2, local copies, waits for them, and re-layouts: 0.03 us -> 3.77 us
    slice x4 -> x0, other arithmetic: 2.55 us -> none  [the longest x3 1.39 us: extended_2(): last = lax.slice_in_dim(value, length - width, length, axis=dim)]
    sub x1 -> x0, other arithmetic: 1.53 us -> none  [body(): residual = source + prior - applied]
    concatenate x4 -> x0, other arithmetic: 1.02 us -> none  [extended_2(): value = jnp.concatenate([before, value, after], axis=dim)]
  transfers between devices with their start and end apart: 11 -> 0, of which waited for: 6 -> 0; matrix products, arithmetic and copies ran while one was open for 3% -> 0% of each run, Pallas kernels for 0% -> 0%
where the time goes in v1:
time: 48.2 us; the launch traced here: 47.9 us
  Pallas kernels  43.5 us (90%)
  local copies, waits for them, and re-layouts  3.77 us (8%)
  between operations  0.64 us (1%)
    pallas_call x1, Pallas kernels, body(): pl.pallas_call(functools.partial(kernel, planes, steps, sends), out_shape...  43.5 us
    unnamed x2, local copies, waits for them, and re-layouts  3.77 us

profile of v1, /device:TPU:0, one launch (start us, length us, event | category | flops | bytes accessed | tf_op | source)
XLA Modules:
  0.0 47.9 jit_solution(8099111848138418968)
XLA Ops:
  0.6 43.5 %smooth.1 = (f32[1,16,64,128]{3,2,1,0:T(8,128)}, f32[1,16,64,128]{3,2,1,0:T(8,128)}) custom-call(f32[1,16,64,128]{3,2,1,0:T(8,128)} %initial.1, f32[1,16,64,128]{3,2,1,0:T(8,128)} %source.1, f32[16,64,128]{2,1,0:T(8,128)} %diffusion.1, f32[3,16,64,128]{3,2,1,0:T(8,128)} %advection.1), custom_call_target="tpu_custom_call" | custom-call | tf_op jit(solution)/shard_map/smooth/pallas_call | solution.py:244
  44.2 1.9 %copy.8 = f32[1,16,64,128]{3,2,1,0:T(8,128)} copy(f32[1,16,64,128]{3,2,1,0:T(8,128)} %get-tuple-element.4) | data formatting | bytes 1048576
  46.1 1.9 %copy.9 = f32[1,16,64,128]{3,2,1,0:T(8,128)} copy(f32[1,16,64,128]{3,2,1,0:T(8,128)} %get-tuple-element.5) | data formatting | bytes 1048576

commit v2 on v1

--- a/solution.py
+++ b/solution.py
@@ -28,10 +28,10 @@
     return first, second, third
 
 
-def kernel(planes, steps, sends, initial, source, diffusion, advection, smoothed, residual,
-           v0, v1, v2, v3, s1, s2, src, p1, p2, p3, spread, upwind,
-           low_z, high_z, low_x, high_x, low_y, high_y, inverse, diagonal, forced, left,
-           load_sem, out_sem, send1, recv1, send2, recv2, send3, recv3, hsend, hrecv):
+def kernel(planes, steps, sends, initial, source, diffusion, advection, s2, left, p3,
+           v0, v1, v2, v3, s1, src, p1, p2, spread, upwind,
+           low_z, high_z, low_x, high_x, low_y, high_y, inverse, diagonal, forced,
+           load_sem, send1, recv1, send2, recv2, send3, recv3, hsend, hrecv):
     first, second, third = sends
     time, side = lax.axis_index("tm"), lax.axis_index("space")
     after, before = lax.rem(time + 1, steps), lax.rem(time + steps - 1, steps)
@@ -48,7 +48,7 @@
         return pl.ds(begin(lo, hi) - HALO, hi - lo)
 
     barrier = pltpu.get_barrier_semaphore()
-    for peer in ((after, side), (before, side), (time, other)):
+    for peer in ((before, side), (time, other)):
         pl.semaphore_signal(barrier, inc=1, device_id=peer, device_id_type=MESH)
 
     inner = pl.ds(HALO, planes)
@@ -99,7 +99,7 @@
     ]
     rim_p1, rim_s1, rim_p2, rim_s2 = rim(p1, near, 4), rim(s1, HALO, 5), rim(p2, near, 6), rim(s2, 1, 7)
 
-    pl.semaphore_wait(barrier, 3)
+    pl.semaphore_wait(barrier, 2)
     sent1[0].start()
     for copy in rims:
         copy.start()
@@ -178,11 +178,9 @@
 
     issued = {"s1": 0, "s2": 0, "rim": set()}
 
-    def issue(name, copies, ranges, ready, extra=None):
+    def issue(name, copies, ranges, ready):
         while issued[name] < len(ranges) and ranges[issued[name]][1] <= ready:
             copies[issued[name]].start()
-            if extra is not None:
-                extra[issued[name]].start()
             issued[name] += 1
 
     def first_ready(ready):
@@ -191,16 +189,11 @@
             rim_s1.start()
         issue("s1", sent2, second, ready)
 
-    outs = [
-        pltpu.make_async_copy(s2.at[span(lo, hi)], smoothed.at[0, grid_span(lo, hi)], out_sem.at[0, k])
-        for k, (lo, hi) in enumerate(third)
-    ]
-
     def second_ready(ready):
         if ready >= 1 and "s2" not in issued["rim"]:
             issued["rim"].add("s2")
             rim_s2.start()
-        issue("s2", sent3, third, ready, outs)
+        issue("s2", sent3, third, ready)
 
     sweep(v0, s1, p1, sent1, first, rim_p1, first_ready)
     rim_s1.wait_recv()
@@ -212,22 +205,23 @@
 
     each(0, planes, partial)
 
-    ends = [
-        pltpu.make_async_copy(left.at[span(lo, hi)], residual.at[0, grid_span(lo, hi)], out_sem.at[1, k])
-        for k, (lo, hi) in enumerate(third)
-    ]
-    for k, (lo, hi) in enumerate(third):
-        sent3[k].wait_recv()
-
-        def finish(i):
-            left[i] = left[i] + p3[i]
-
-        each(lo, hi, finish)
-        ends[k].start()
-
+    for copy in sent3:
+        copy.wait_recv()
     for copy in rims + [rim_p1, rim_s1, rim_p2, rim_s2] + sent1 + sent2 + sent3:
         copy.wait_send()
-    for copy in outs + ends:
+
+
+def finish(planes, step, s2, left, p3, smoothed, residual, total, sem):
+    out = pltpu.make_async_copy(s2.at[pl.ds(HALO, planes)], smoothed.at[0], sem.at[0])
+    out.start()
+    copies = [out]
+    for k, lo in enumerate(range(0, planes, step)):
+        size = min(step, planes - lo)
+        part, wide = pl.ds(lo, size), pl.ds(HALO + lo, size)
+        total[part] = left[wide] + p3[wide]
+        copies.append(pltpu.make_async_copy(total.at[part], residual.at[0, part], sem.at[1 + k]))
+        copies[-1].start()
+    for copy in copies:
         copy.wait()
 
 
@@ -235,22 +229,34 @@
     assert sides == 2
     _, planes, rows, lanes = initial.shape
     sends = plan(planes, 4)
-    most = max(len(s) for s in sends)
-    wide = pltpu.VMEM((planes + 2 * HALO, rows, lanes), jnp.float32)
-    triple = pltpu.VMEM((3, planes + 2 * HALO, rows, lanes), jnp.float32)
+    shape = (planes + 2 * HALO, rows, lanes)
+    wide = pltpu.VMEM(shape, jnp.float32)
+    triple = pltpu.VMEM((3,) + shape, jnp.float32)
     dma = pltpu.SemaphoreType.DMA
     pairs = [dma((len(s),)) for s in sends for _ in range(2)]
     result = jax.ShapeDtypeStruct(initial.shape, jnp.float32)
-    return pl.pallas_call(
+    vmem = pl.BlockSpec(memory_space=pltpu.VMEM)
+    hbm = pl.BlockSpec(memory_space=pltpu.HBM)
+    held = pl.pallas_call(
         functools.partial(kernel, planes, steps, sends),
-        out_shape=(result, result),
-        in_specs=[pl.BlockSpec(memory_space=pl.ANY)] * 4,
-        out_specs=(pl.BlockSpec(memory_space=pl.ANY),) * 2,
-        scratch_shapes=[wide] * 11 + [triple] + [wide] * 10
-        + [dma((4,)), dma((2, most))] + pairs + [dma((8,)), dma((8,))],
-        compiler_params=pltpu.CompilerParams(collective_id=0, has_side_effects=True),
+        out_shape=(wide,) * 3,
+        in_specs=[hbm] * 4,
+        out_specs=(vmem,) * 3,
+        scratch_shapes=[wide] * 9 + [triple] + [wide] * 9
+        + [dma((4,))] + pairs + [dma((8,)), dma((8,))],
+        compiler_params=pltpu.CompilerParams(collective_id=0, has_side_effects=True, vmem_limit_bytes=40 << 20),
         name="smooth",
     )(initial, source, diffusion, advection)
+    step = 4
+    return pl.pallas_call(
+        functools.partial(finish, planes, step),
+        out_shape=(result, result),
+        in_specs=[vmem] * 3,
+        out_specs=(hbm,) * 2,
+        scratch_shapes=[pltpu.VMEM((planes, rows, lanes), jnp.float32), dma((1 + -(-planes // step),))],
+        compiler_params=pltpu.CompilerParams(vmem_limit_bytes=8 << 20),
+        name="finish",
+    )(*held)
 
 
 def solution(mesh):

time: 48.2 us -> 49 us (1.017)
  local copies, waits for them, and re-layouts: 3.77 us -> 4.52 us
    pallas_call x0 -> x1, Pallas kernels: none -> 1 us  [body(): pl.pallas_call(functools.partial(finish, planes, step), out_shape=(result...]
    pallas_call x1, Pallas kernels: 43.5 us -> 42.5 us  [body(): pl.pallas_call(functools.partial(kernel, planes, steps, sends), out_shape...]
    unnamed x2 -> x8, local copies, waits for them, and re-layouts: 3.77 us -> 4.52 us
where the time goes in v2:
time: 49 us; the launch traced here: 48.7 us
  Pallas kernels  43.5 us (89%)
  local copies, waits for them, and re-layouts  4.52 us (9%)
  between operations  0.65 us (1%)
    pallas_call x1, Pallas kernels, body(): pl.pallas_call(functools.partial(kernel, planes, steps, sends), out_shape...  42.5 us
    unnamed x8, local copies, waits for them, and re-layouts  4.52 us
    pallas_call x1, Pallas kernels, body(): pl.pallas_call(functools.partial(finish, planes, step), out_shape=(result...  1 us

profile of v2, /device:TPU:0, one launch (start us, length us, event | category | flops | bytes accessed | tf_op | source)
XLA Modules:
  0.0 48.7 jit_solution(15237216132929548200)
XLA Ops:
  0.6 0.0 copy-start
  0.6 1.4 %copy-done = f32[3,16,64,128]{3,2,1,0:T(8,128)S(1)} copy-done((f32[3,16,64,128]{3,2,1,0:T(8,128)S(1)}, f32[3,16,64,128]{3,2,1,0:T(8,128)}, u32[]{:S(2)}) %copy-start) | copy-done | bytes 1572888
  2.0 0.0 copy-start.1
  2.0 1.0 %copy-done.1 = f32[1,16,64,128]{3,2,1,0:T(8,128)S(1)} copy-done((f32[1,16,64,128]{3,2,1,0:T(8,128)S(1)}, f32[1,16,64,128]{3,2,1,0:T(8,128)}, u32[]{:S(2)}) %copy-start.1) | copy-done | bytes 524312
  3.1 0.0 copy-start.2
  3.1 1.0 %copy-done.2 = f32[1,16,64,128]{3,2,1,0:T(8,128)S(1)} copy-done((f32[1,16,64,128]{3,2,1,0:T(8,128)S(1)}, f32[1,16,64,128]{3,2,1,0:T(8,128)}, u32[]{:S(2)}) %copy-start.2) | copy-done | bytes 524312
  4.1 0.0 copy-start.3
  4.1 1.0 %copy-done.3 = f32[16,64,128]{2,1,0:T(8,128)S(1)} copy-done((f32[16,64,128]{2,1,0:T(8,128)S(1)}, f32[16,64,128]{2,1,0:T(8,128)}, u32[]{:S(2)}) %copy-start.3) | copy-done | bytes 524312
  5.2 42.5 %smooth.1 = (f32[24,64,128]{2,1,0:T(8,128)S(1)}, f32[24,64,128]{2,1,0:T(8,128)S(1)}, f32[24,64,128]{2,1,0:T(8,128)S(1)}) custom-call(f32[1,16,64,128]{3,2,1,0:T(8,128)S(1)} %copy-done.1, f32[1,16,64,128]{3,2,1,0:T(8,128)S(1)} %copy-done.2, f32[16,64,128]{2,1,0:T(8,128)S(1)} %copy-done.3, f32[3,16,64,128]{3,2,1,0:T(8,128)S(1)} %copy-done), custom_call_target="tpu_custom_call" | custom-call | tf_op jit(solution)/shard_map/smooth/pallas_call | solution.py:240
  47.7 1.0 %finish.1 = (f32[1,16,64,128]{3,2,1,0:T(8,128)}, f32[1,16,64,128]{3,2,1,0:T(8,128)}) custom-call(f32[24,64,128]{2,1,0:T(8,128)S(1)} %get-tuple-element.5.s2, f32[24,64,128]{2,1,0:T(8,128)S(1)} %get-tuple-element.6.left, f32[24,64,128]{2,1,0:T(8,128)S(1)} %get-tuple-element.7.p3), custom_call_target="tpu_custom_call" | custom-call | tf_op jit(solution)/shard_map/finish/pallas_call | solution.py:251
Async XLA Ops:
  0.6 1.4 %copy-start = (f32[3,16,64,128]{3,2,1,0:T(8,128)S(1)}, f32[3,16,64,128]{3,2,1,0:T(8,128)}, u32[]{:S(2)}) copy-start(f32[3,16,64,128]{3,2,1,0:T(8,128)} %advection.1) | copy-start | bytes 4718596
  2.0 1.0 %copy-start.1 = (f32[1,16,64,128]{3,2,1,0:T(8,128)S(1)}, f32[1,16,64,128]{3,2,1,0:T(8,128)}, u32[]{:S(2)}) copy-start(f32[1,16,64,128]{3,2,1,0:T(8,128)} %initial.1) | copy-start | bytes 1572868
  3.1 1.0 %copy-start.2 = (f32[1,16,64,128]{3,2,1,0:T(8,128)S(1)}, f32[1,16,64,128]{3,2,1,0:T(8,128)}, u32[]{:S(2)}) copy-start(f32[1,16,64,128]{3,2,1,0:T(8,128)} %source.1) | copy-start | bytes 1572868
  4.1 1.0 %copy-start.3 = (f32[16,64,128]{2,1,0:T(8,128)S(1)}, f32[16,64,128]{2,1,0:T(8,128)}, u32[]{:S(2)}) copy-start(f32[16,64,128]{2,1,0:T(8,128)} %diffusion.1) | copy-start | bytes 1572868

commit v3 on v2

--- a/solution.py
+++ b/solution.py
@@ -10,6 +10,7 @@
 SWEEPS = 2
 ITERS = 4
 HALO = ITERS
+VMEM_BYTES = 67043328
 MESH = pl.DeviceIdType.MESH
 
 
@@ -237,6 +238,7 @@
     result = jax.ShapeDtypeStruct(initial.shape, jnp.float32)
     vmem = pl.BlockSpec(memory_space=pltpu.VMEM)
     hbm = pl.BlockSpec(memory_space=pltpu.HBM)
+    grant = VMEM_BYTES - (3 * shape[0] + 4) * rows * lanes * 4
     held = pl.pallas_call(
         functools.partial(kernel, planes, steps, sends),
         out_shape=(wide,) * 3,
@@ -244,7 +246,7 @@
         out_specs=(vmem,) * 3,
         scratch_shapes=[wide] * 9 + [triple] + [wide] * 9
         + [dma((4,))] + pairs + [dma((8,)), dma((8,))],
-        compiler_params=pltpu.CompilerParams(collective_id=0, has_side_effects=True, vmem_limit_bytes=40 << 20),
+        compiler_params=pltpu.CompilerParams(collective_id=0, has_side_effects=True, vmem_limit_bytes=grant),
         name="smooth",
     )(initial, source, diffusion, advection)
     step = 4

time: 49 us -> 44.6 us (0.910)
  local copies, waits for them, and re-layouts: 4.52 us -> 0 us
    unnamed x8 -> x0, local copies, waits for them, and re-layouts: 4.52 us -> none
where the time goes in v3:
time: 44.6 us; the launch traced here: 44.4 us
  Pallas kernels  43.8 us (98%)
  between operations  0.64 us (1%)
    pallas_call x1, Pallas kernels, body(): pl.pallas_call(functools.partial(kernel, planes, steps, sends), out_shape...  42.8 us
    pallas_call x1, Pallas kernels, body(): pl.pallas_call(functools.partial(finish, planes, step), out_shape=(result...  1 us

profile of v3, /device:TPU:0, one launch (start us, length us, event | category | flops | bytes accessed | tf_op | source)
XLA Modules:
  0.0 44.4 jit_solution(1171554435407945485)
XLA Ops:
  0.6 42.8 %smooth.1 = (f32[24,64,128]{2,1,0:T(8,128)S(1)}, f32[24,64,128]{2,1,0:T(8,128)S(1)}, f32[24,64,128]{2,1,0:T(8,128)S(1)}) custom-call(f32[1,16,64,128]{3,2,1,0:T(8,128)} %initial.1, f32[1,16,64,128]{3,2,1,0:T(8,128)} %source.1, f32[16,64,128]{2,1,0:T(8,128)} %diffusion.1, f32[3,16,64,128]{3,2,1,0:T(8,128)} %advection.1), custom_call_target="tpu_custom_call" | custom-call | tf_op jit(solution)/shard_map/smooth/pallas_call | solution.py:242
  43.4 1.0 %finish.1 = (f32[1,16,64,128]{3,2,1,0:T(8,128)}, f32[1,16,64,128]{3,2,1,0:T(8,128)}) custom-call(f32[24,64,128]{2,1,0:T(8,128)S(1)} %get-tuple-element.5.s2, f32[24,64,128]{2,1,0:T(8,128)S(1)} %get-tuple-element.6.left, f32[24,64,128]{2,1,0:T(8,128)S(1)} %get-tuple-element.7.p3), custom_call_target="tpu_custom_call" | custom-call | tf_op jit(solution)/shard_map/finish/pallas_call | solution.py:253

commit v4 on v3

--- a/solution.py
+++ b/solution.py
@@ -23,16 +23,18 @@
     ready = lambda edges: [e if e == planes else max(e - (ITERS - 1), 0) for e in edges]
     split = lambda edges, most: sorted({c for a, b in cuts(edges) for c in list(range(a, b, most)) + [b]})
     first = cuts(arrive)
+    lo, hi = first[-1]
+    first = first[:-1] + [(lo, (lo + hi) // 2), ((lo + hi) // 2, hi)]
     second = cuts(split(sorted(set(ready(arrive))), step))
     edges = [0] + [b for _, b in second]
     third = cuts(split(sorted(set(ready(edges))), 2))
     return first, second, third
 
 
-def kernel(planes, steps, sends, initial, source, diffusion, advection, s2, left, p3,
+def kernel(planes, steps, sends, relays, initial, source, diffusion, advection, s2, left, p3,
            v0, v1, v2, v3, s1, src, p1, p2, spread, upwind,
            low_z, high_z, low_x, high_x, low_y, high_y, inverse, diagonal, forced,
-           load_sem, send1, recv1, send2, recv2, send3, recv3, hsend, hrecv):
+           held, load_sem, send1, recv1, send2, recv2, send3, recv3, hsend, hrecv, rsend, rrecv):
     first, second, third = sends
     time, side = lax.axis_index("tm"), lax.axis_index("space")
     after, before = lax.rem(time + 1, steps), lax.rem(time + steps - 1, steps)
@@ -51,6 +53,18 @@
     barrier = pltpu.get_barrier_semaphore()
     for peer in ((before, side), (time, other)):
         pl.semaphore_signal(barrier, inc=1, device_id=peer, device_id_type=MESH)
+    last = steps - 1
+    greeted = 2
+    for stop, _ in relays:
+        @pl.when(time == 0)
+        def _():
+            pl.semaphore_signal(barrier, inc=1, device_id=(stop, side), device_id_type=MESH)
+
+        @pl.when(time == stop)
+        def _():
+            pl.semaphore_signal(barrier, inc=1, device_id=(last, side), device_id_type=MESH)
+
+        greeted += jnp.where((time == stop) | (time == last), 1, 0)
 
     inner = pl.ds(HALO, planes)
     loads = [
@@ -100,12 +114,41 @@
     ]
     rim_p1, rim_s1, rim_p2, rim_s2 = rim(p1, near, 4), rim(s1, HALO, 5), rim(p2, near, 6), rim(s2, 1, 7)
 
-    pl.semaphore_wait(barrier, 2)
+    pl.semaphore_wait(barrier, greeted)
+    relayed = {chunk: (n, stop) for n, (stop, chunk) in enumerate(relays)}
+    outward, onward = {}, {}
+    for chunk, (n, stop) in relayed.items():
+        lo, hi = first[chunk]
+        room = held.at[n, pl.ds(0, hi - lo)]
+        outward[chunk] = pltpu.make_async_remote_copy(
+            src_ref=initial.at[0, grid_span(lo, hi)], dst_ref=room, send_sem=send1.at[chunk],
+            recv_sem=rrecv.at[n], device_id=(stop, side), device_id_type=MESH)
+        onward[chunk] = pltpu.make_async_remote_copy(
+            src_ref=room, dst_ref=p1.at[span(lo, hi)], send_sem=rsend.at[n],
+            recv_sem=recv1.at[chunk], device_id=(0, side), device_id_type=MESH)
+
     sent1[0].start()
     for copy in rims:
         copy.start()
-    for copy in sent1[1:]:
-        copy.start()
+    for chunk in relayed:
+        @pl.when(time == last)
+        def _():
+            outward[chunk].start()
+
+    for chunk, copy in enumerate(sent1):
+        if chunk in relayed:
+            @pl.when(time != last)
+            def _():
+                copy.start()
+        elif chunk > 0:
+            copy.start()
+
+    def pass_on():
+        for chunk, (n, stop) in relayed.items():
+            @pl.when(time == stop)
+            def _():
+                outward[chunk].wait_recv()
+                onward[chunk].start()
 
     def each(lo, hi, body):
         if hi > lo:
@@ -188,6 +231,9 @@
         if ready >= HALO and "s1" not in issued["rim"]:
             issued["rim"].add("s1")
             rim_s1.start()
+        if "relay" not in issued["rim"]:
+            issued["rim"].add("relay")
+            pass_on()
         issue("s1", sent2, second, ready)
 
     def second_ready(ready):
@@ -210,6 +256,10 @@
         copy.wait_recv()
     for copy in rims + [rim_p1, rim_s1, rim_p2, rim_s2] + sent1 + sent2 + sent3:
         copy.wait_send()
+    for chunk, (n, stop) in relayed.items():
+        @pl.when(time == stop)
+        def _():
+            onward[chunk].wait_send()
 
 
 def finish(planes, step, s2, left, p3, smoothed, residual, total, sem):
@@ -230,6 +280,9 @@
     assert sides == 2
     _, planes, rows, lanes = initial.shape
     sends = plan(planes, 4)
+    chunks = len(sends[0])
+    relays = [(steps // 4 - 1, chunks - 2), (steps - 3, chunks - 1)] if steps >= 8 else []
+    most = max(hi - lo for lo, hi in sends[0])
     shape = (planes + 2 * HALO, rows, lanes)
     wide = pltpu.VMEM(shape, jnp.float32)
     triple = pltpu.VMEM((3,) + shape, jnp.float32)
@@ -240,12 +293,13 @@
     hbm = pl.BlockSpec(memory_space=pltpu.HBM)
     grant = VMEM_BYTES - (3 * shape[0] + 4) * rows * lanes * 4
     held = pl.pallas_call(
-        functools.partial(kernel, planes, steps, sends),
+        functools.partial(kernel, planes, steps, sends, relays),
         out_shape=(wide,) * 3,
         in_specs=[hbm] * 4,
         out_specs=(vmem,) * 3,
         scratch_shapes=[wide] * 9 + [triple] + [wide] * 9
-        + [dma((4,))] + pairs + [dma((8,)), dma((8,))],
+        + [pltpu.VMEM((max(len(relays), 1), most, rows, lanes), jnp.float32)]
+        + [dma((4,))] + pairs + [dma((8,))] * 2 + [dma((max(len(relays), 1),))] * 2,
         compiler_params=pltpu.CompilerParams(collective_id=0, has_side_effects=True, vmem_limit_bytes=grant),
         name="smooth",
     )(initial, source, diffusion, advection)

time: 44.6 us -> 63.1 us (1.41)
  Pallas kernels: 43.8 us -> 62.3 us
    pallas_call x1, Pallas kernels: 42.8 us -> 61.3 us  [body(): pl.pallas_call(functools.partial(kernel, planes, steps, sends, relays), o...]
where the time goes in v4:
time: 63.1 us; the launch traced here: 63 us
  Pallas kernels  62.3 us (99%)
  between operations  0.64 us (1%)
    pallas_call x1, Pallas kernels, body(): pl.pallas_call(functools.partial(kernel, planes, steps, sends, relays), o...  61.3 us

profile of v4, /device:TPU:0, one launch (start us, length us, event | category | flops | bytes accessed | tf_op | source)
XLA Modules:
  0.0 63.0 jit_solution(9202115497442630675)
XLA Ops:
  0.6 61.3 %smooth.1 = (f32[24,64,128]{2,1,0:T(8,128)S(1)}, f32[24,64,128]{2,1,0:T(8,128)S(1)}, f32[24,64,128]{2,1,0:T(8,128)S(1)}) custom-call(f32[1,16,64,128]{3,2,1,0:T(8,128)} %initial.1, f32[1,16,64,128]{3,2,1,0:T(8,128)} %source.1, f32[16,64,128]{2,1,0:T(8,128)} %diffusion.1, f32[3,16,64,128]{3,2,1,0:T(8,128)} %advection.1), custom_call_target="tpu_custom_call" | custom-call | tf_op jit(solution)/shard_map/smooth/pallas_call | solution.py:295
  62.0 1.0 %finish.1 = (f32[1,16,64,128]{3,2,1,0:T(8,128)}, f32[1,16,64,128]{3,2,1,0:T(8,128)}) custom-call(f32[24,64,128]{2,1,0:T(8,128)S(1)} %get-tuple-element.5.s2, f32[24,64,128]{2,1,0:T(8,128)S(1)} %get-tuple-element.6.left, f32[24,64,128]{2,1,0:T(8,128)S(1)} %get-tuple-element.7.p3), custom_call_target="tpu_custom_call" | custom-call | tf_op jit(solution)/shard_map/finish/pallas_call | solution.py:307

commit v5 on v4

--- a/solution.py
+++ b/solution.py
@@ -24,7 +24,7 @@
     split = lambda edges, most: sorted({c for a, b in cuts(edges) for c in list(range(a, b, most)) + [b]})
     first = cuts(arrive)
     lo, hi = first[-1]
-    first = first[:-1] + [(lo, (lo + hi) // 2), ((lo + hi) // 2, hi)]
+    first = first[:-1] + [(lo, hi - 3), (hi - 3, hi)]
     second = cuts(split(sorted(set(ready(arrive))), step))
     edges = [0] + [b for _, b in second]
     third = cuts(split(sorted(set(ready(edges))), 2))
@@ -281,7 +281,7 @@
     _, planes, rows, lanes = initial.shape
     sends = plan(planes, 4)
     chunks = len(sends[0])
-    relays = [(steps // 4 - 1, chunks - 2), (steps - 3, chunks - 1)] if steps >= 8 else []
+    relays = [(steps - 2, chunks - 1)] if steps >= 8 else []
     most = max(hi - lo for lo, hi in sends[0])
     shape = (planes + 2 * HALO, rows, lanes)
     wide = pltpu.VMEM(shape, jnp.float32)

time: 63.1 us -> 69.8 us (1.11)
  Pallas kernels: 62.3 us -> 69 us
    pallas_call x1, Pallas kernels: 61.3 us -> 68 us  [body(): pl.pallas_call(functools.partial(kernel, planes, steps, sends, relays), o...]
where the time goes in v5:
time: 69.8 us; the launch traced here: 69.6 us
  Pallas kernels  69 us (99%)
    pallas_call x1, Pallas kernels, body(): pl.pallas_call(functools.partial(kernel, planes, steps, sends, relays), o...  68 us

profile of v5, /device:TPU:0, one launch (start us, length us, event | category | flops | bytes accessed | tf_op | source)
XLA Modules:
  0.0 69.6 jit_solution(2866204924839619634)
XLA Ops:
  0.6 68.0 %smooth.1 = (f32[24,64,128]{2,1,0:T(8,128)S(1)}, f32[24,64,128]{2,1,0:T(8,128)S(1)}, f32[24,64,128]{2,1,0:T(8,128)S(1)}) custom-call(f32[1,16,64,128]{3,2,1,0:T(8,128)} %initial.1, f32[1,16,64,128]{3,2,1,0:T(8,128)} %source.1, f32[16,64,128]{2,1,0:T(8,128)} %diffusion.1, f32[3,16,64,128]{3,2,1,0:T(8,128)} %advection.1), custom_call_target="tpu_custom_call" | custom-call | tf_op jit(solution)/shard_map/smooth/pallas_call | solution.py:295
  68.6 1.0 %finish.1 = (f32[1,16,64,128]{3,2,1,0:T(8,128)}, f32[1,16,64,128]{3,2,1,0:T(8,128)}) custom-call(f32[24,64,128]{2,1,0:T(8,128)S(1)} %get-tuple-element.5.s2, f32[24,64,128]{2,1,0:T(8,128)S(1)} %get-tuple-element.6.left, f32[24,64,128]{2,1,0:T(8,128)S(1)} %get-tuple-element.7.p3), custom_call_target="tpu_custom_call" | custom-call | tf_op jit(solution)/shard_map/finish/pallas_call | solution.py:307

commit v6 on v3

--- a/solution.py
+++ b/solution.py
@@ -59,7 +59,7 @@
         pltpu.make_async_copy(source.at[0], src.at[inner], load_sem.at[2]),
         pltpu.make_async_copy(initial.at[0], v0.at[inner], load_sem.at[3]),
     ]
-    for load in loads:
+    for load in loads[::-1]:
         load.start()
 
     edge = begin(planes, planes + 1)
@@ -81,7 +81,7 @@
 
     near = HALO - 1
     sent1 = [
-        forward(initial.at[0, grid_span(lo, hi)], p1.at[span(lo, hi)], send1.at[k], recv1.at[k])
+        forward(v0.at[span(lo, hi)], p1.at[span(lo, hi)], send1.at[k], recv1.at[k])
         for k, (lo, hi) in enumerate(first)
     ]
     sent2 = [
@@ -101,6 +101,7 @@
     rim_p1, rim_s1, rim_p2, rim_s2 = rim(p1, near, 4), rim(s1, HALO, 5), rim(p2, near, 6), rim(s2, 1, 7)
 
     pl.semaphore_wait(barrier, 2)
+    loads[3].wait()
     sent1[0].start()
     for copy in rims:
         copy.start()
@@ -173,8 +174,8 @@
         loads[n].wait()
         rims[n].wait_recv()
     each(-near, planes, coefficients)
+    loads[2].wait()
     for n in (2, 3):
-        loads[n].wait()
         rims[n].wait_recv()
 
     issued = {"s1": 0, "s2": 0, "rim": set()}

time: 44.6 us -> 44.7 us (level)
  no operation moved by 1% of the time
where the time goes in v6:
time: 44.7 us; the launch traced here: 44.6 us
  Pallas kernels  43.9 us (98%)
  between operations  0.64 us (1%)
    pallas_call x1, Pallas kernels, body(): pl.pallas_call(functools.partial(kernel, planes, steps, sends), out_shape...  42.9 us
    pallas_call x1, Pallas kernels, body(): pl.pallas_call(functools.partial(finish, planes, step), out_shape=(result...  1 us

profile of v6, /device:TPU:0, one launch (start us, length us, event | category | flops | bytes accessed | tf_op | source)
XLA Modules:
  0.0 44.6 jit_solution(17306326656295346356)
XLA Ops:
  0.6 42.9 %smooth.1 = (f32[24,64,128]{2,1,0:T(8,128)S(1)}, f32[24,64,128]{2,1,0:T(8,128)S(1)}, f32[24,64,128]{2,1,0:T(8,128)S(1)}) custom-call(f32[1,16,64,128]{3,2,1,0:T(8,128)} %initial.1, f32[1,16,64,128]{3,2,1,0:T(8,128)} %source.1, f32[16,64,128]{2,1,0:T(8,128)} %diffusion.1, f32[3,16,64,128]{3,2,1,0:T(8,128)} %advection.1), custom_call_target="tpu_custom_call" | custom-call | tf_op jit(solution)/shard_map/smooth/pallas_call | solution.py:243
  43.6 1.0 %finish.1 = (f32[1,16,64,128]{3,2,1,0:T(8,128)}, f32[1,16,64,128]{3,2,1,0:T(8,128)}) custom-call(f32[24,64,128]{2,1,0:T(8,128)S(1)} %get-tuple-element.5.s2, f32[24,64,128]{2,1,0:T(8,128)S(1)} %get-tuple-element.6.left, f32[24,64,128]{2,1,0:T(8,128)S(1)} %get-tuple-element.7.p3), custom_call_target="tpu_custom_call" | custom-call | tf_op jit(solution)/shard_map/finish/pallas_call | solution.py:254
